TPU v7x, 32 devices: a whole 2x2x4 slice. The times are simulated.
32 devices in a mesh: dp: 16 (over z, x, core), tensor: 2 (over y).
Axes of the slice: x: 2, y: 2, z: 4, core: 2. Of those that a mesh axis runs over, the one named last changes fastest.
Arguments:
- inputs: bfloat16 [2, 16, 1024, 768], P(None, 'dp', 'tensor'), may hold values from -6 to 6
- seg_ids: int32 [2, 16, 1024], P(None, 'dp'), may hold values from 0 to 7, never falling along the last dimension, each value on 1 to 512 neighbouring positions
- keep_mask: int32 [2, 16, 1024], P(None, 'dp'), may hold values 0 or 1
- w_qkv: bfloat16 [3, 768, 768], P(None, 'dp', 'tensor'), may hold values from -0.21875 to 0.21875
- b_qv: float32 [2, 768], replicated, may hold values from -3 to 3
- w_o: bfloat16 [768, 768], P('tensor', 'dp'), may hold values from -1.75 to 1.75
- b_o: float32 [768], replicated, may hold values from -3 to 3
- gain_one: float32 [768], replicated, may hold values from 0.5 to 1.5
- shift_one: float32 [768], replicated, may hold values from -3 to 3
- w_up: bfloat16 [768, 3072], P('dp', 'tensor'), may hold values from -0.21875 to 0.21875
- b_up: float32 [3072], replicated, may hold values from -3 to 3
- w_down: bfloat16 [3072, 768], P('tensor', 'dp'), may hold values from -0.109375 to 0.109375
- b_down: float32 [768], replicated, may hold values from -3 to 3
- gain_two: float32 [768], replicated, may hold values from 0.5 to 1.5
- shift_two: float32 [768], replicated, may hold values from -3 to 3
- out_grad: bfloat16 [2, 16, 1024, 768], P(None, 'dp', 'tensor'), may hold values from -6 to 6
Outputs:
- out: bfloat16 [2, 16, 1024, 768], P(None, 'dp', 'tensor')
- x_grad: float32 [2, 16, 1024, 768], P(None, 'dp', 'tensor')
- w_qkv_grad: float32 [3, 768, 768], P(None, 'dp', 'tensor')
- b_qv_grad: float32 [2, 768], P(None, 'tensor')
- w_o_grad: float32 [768, 768], P('tensor', 'dp')
- b_o_grad: float32 [768], replicated
- gain_one_grad: float32 [768], replicated
- shift_one_grad: float32 [768], replicated
- w_up_grad: float32 [768, 3072], P('dp', 'tensor')
- b_up_grad: float32 [3072], P('tensor')
- w_down_grad: float32 [3072, 768], P('tensor', 'dp')
- b_down_grad: float32 [768], replicated
- gain_two_grad: float32 [768], replicated
- shift_two_grad: float32 [768], replicated
Inputs may be any that keep to these rules, and one draw needn't show every extreme that they name: `seg_ids`: within each sequence of 1024 positions the document numbers never fall; each document holds 1 to 512 positions and one holds exactly 512.
All inputs are finite; a program needn't handle non-finite values. No bound on the sum of `keep_mask` on one device may be relied on, other than what follows from the above.
Results may differ from a plain program's by a relative error of at most 0.015.
Values may be sent and summed in bfloat16 or wider, within the bound.
A program may use at most 192 MiB of HBM per device.

v0:
```python
import math
import jax
import jax.numpy as jnp
from jax import lax
from jax.sharding import PartitionSpec as P

HEAD_DIM = 64
EPS = 1e-06


def gelu_exact(v):
    return 0.5 * v * (1.0 + lax.erf(v * 0.7071067811865476))


def gelu_slope(v):
    return (
        0.5 * (1.0 + lax.erf(v * 0.7071067811865476))
        + v * jnp.exp(-0.5 * v * v) * 0.3989422804014327
    )


def norm_rows(v, gain, shift):
    row_mean = jnp.mean(v, axis=-1, keepdims=True)
    centered = v - row_mean
    factor = lax.rsqrt(jnp.mean(centered * centered, axis=-1, keepdims=True) + EPS)
    normed = centered * factor
    return (normed * gain + shift, normed, factor)


def norm_back(grad_rows, normed, factor, gain):
    inner = grad_rows * gain
    return factor * (
        inner
        - jnp.mean(inner, axis=-1, keepdims=True)
        - normed * jnp.mean(inner * normed, axis=-1, keepdims=True)
    )


def allowed_keys(seg_block, seg_full, keep_full, row_start):
    shape_pair = (seg_block.shape[0], seg_full.shape[0])
    own_pos = row_start + lax.broadcasted_iota(jnp.int32, shape_pair, 0)
    key_pos = lax.broadcasted_iota(jnp.int32, shape_pair, 1)
    return (seg_block[:, None] == seg_full[None, :]) & (
        (keep_full[None, :] == 1) | (own_pos == key_pos)
    )


def block_scores(q_rows, key_rows, allowed, score_scale):
    raw = (
        jnp.einsum("qhd,khd->hqk", q_rows, key_rows, preferred_element_type=jnp.float32)
        * score_scale
    )
    return jnp.where(allowed[None], raw, -1e30)


def attend(queries, key_rows, values, seg_full, keep_full, score_scale, block_rows):
    length, head_count, head_width = queries.shape
    block_count = length // block_rows
    starts = jnp.arange(block_count, dtype=jnp.int32) * block_rows

    def per_block(block_item):
        q_rows, seg_block, row_start = block_item
        scores = block_scores(
            q_rows, key_rows, allowed_keys(seg_block, seg_full, keep_full, row_start), score_scale
        )
        row_max = jnp.max(scores, axis=-1, keepdims=True)
        exps_rows = jnp.exp(scores - row_max)
        denom = jnp.sum(exps_rows, axis=-1, keepdims=True)
        low_probs = (exps_rows / denom).astype(jnp.bfloat16)
        context = jnp.einsum("hqk,khd->qhd", low_probs, values, preferred_element_type=jnp.float32)
        return (context.astype(jnp.bfloat16), (row_max + jnp.log(denom))[..., 0])

    context, logsum = lax.map(
        per_block,
        (
            queries.reshape(block_count, block_rows, head_count, head_width),
            seg_full.reshape(block_count, block_rows),
            starts,
        ),
    )
    return (context.reshape(length, head_count * head_width), logsum)


def attend_back(
    queries, key_rows, values, grad_context, logsum, seg_full, keep_full, score_scale, block_rows
):
    length, head_count, head_width = queries.shape
    block_count = length // block_rows
    starts = jnp.arange(block_count, dtype=jnp.int32) * block_rows

    def per_block(carried, block_item):
        key_acc, value_acc = carried
        q_rows, g_rows, lse_rows, seg_block, row_start = block_item
        scores = block_scores(
            q_rows, key_rows, allowed_keys(seg_block, seg_full, keep_full, row_start), score_scale
        )
        probs = jnp.exp(scores - lse_rows[..., None])
        low_probs = probs.astype(jnp.bfloat16)
        grad_probs = jnp.einsum("qhd,khd->hqk", g_rows, values, preferred_element_type=jnp.float32)
        inner = jnp.sum(probs * grad_probs, axis=-1, keepdims=True)
        grad_scores = (probs * (grad_probs - inner)).astype(jnp.bfloat16)
        grad_q = (
            jnp.einsum("hqk,khd->qhd", grad_scores, key_rows, preferred_element_type=jnp.float32)
            * score_scale
        )
        key_acc = (
            key_acc
            + jnp.einsum("hqk,qhd->khd", grad_scores, q_rows, preferred_element_type=jnp.float32)
            * score_scale
        )
        value_acc = value_acc + jnp.einsum(
            "hqk,qhd->khd", low_probs, g_rows, preferred_element_type=jnp.float32
        )
        return ((key_acc, value_acc), grad_q.astype(jnp.bfloat16))

    zero_grad = jnp.zeros((length, head_count, head_width), jnp.float32)
    grad_ctx4 = grad_context.reshape(block_count, block_rows, head_count, head_width)
    (key_acc, value_acc), grad_q = lax.scan(
        per_block,
        (zero_grad, zero_grad),
        (
            queries.reshape(block_count, block_rows, head_count, head_width),
            grad_ctx4,
            logsum,
            seg_full.reshape(block_count, block_rows),
            starts,
        ),
    )
    flat = head_count * head_width
    return (
        grad_q.reshape(length, flat),
        key_acc.reshape(length, flat).astype(jnp.bfloat16),
        value_acc.reshape(length, flat).astype(jnp.bfloat16),
    )


def add_all(left, right):
    return tuple((a + b for a, b in zip(left, right)))


def shards(
    inputs,
    seg_ids,
    keep_mask,
    w_qkv,
    b_qv,
    w_o,
    b_o,
    gain_one,
    shift_one,
    w_up,
    b_up,
    w_down,
    b_down,
    gain_two,
    shift_two,
    out_grad,
):
    micro_count = inputs.shape[0]
    own_count = inputs.shape[2]
    half_width = w_qkv.shape[2]
    half_units = w_up.shape[1]
    score_scale = 1.0 / math.sqrt(HEAD_DIM)
    tensor_count = lax.axis_size("tensor")
    tensor_rank = lax.axis_index("tensor")
    length = own_count * tensor_count
    block_rows = min(512, length)
    bias_qv = lax.dynamic_slice_in_dim(b_qv, tensor_rank * half_width, half_width, 1)
    bias_up = lax.dynamic_slice_in_dim(b_up, tensor_rank * half_units, half_units, 0)
    shard_grads = None
    local_totals = None
    small_totals = None
    out_list = []
    grad_list = []
    for micro_index in range(micro_count):
        own_rows = inputs[micro_index, 0]
        seg_full = seg_ids[micro_index, 0]
        keep_full = keep_mask[micro_index, 0]
        full_qkv = lax.all_gather(w_qkv, "dp", axis=1, tiled=True)
        full_o = lax.all_gather(w_o, "dp", axis=1, tiled=True)
        full_up = lax.all_gather(w_up, "dp", axis=0, tiled=True)
        full_down = lax.all_gather(w_down, "dp", axis=1, tiled=True)
        head_count = full_qkv.shape[2] // HEAD_DIM
        gathered = lax.all_gather(own_rows, "tensor", axis=0, tiled=True)
        projected = jnp.einsum(
            "ld,cde->cle", gathered, full_qkv, preferred_element_type=jnp.float32
        )
        bias_rows = jnp.stack([bias_qv[0], jnp.zeros_like(bias_qv[0]), bias_qv[1]])
        projected = (projected + bias_rows[:, None, :]).astype(jnp.bfloat16)
        queries = projected[0].reshape(length, head_count, HEAD_DIM)
        key_rows = projected[1].reshape(length, head_count, HEAD_DIM)
        values = projected[2].reshape(length, head_count, HEAD_DIM)
        context, logsum = attend(
            queries, key_rows, values, seg_full, keep_full, score_scale, block_rows
        )
        attn_rows = lax.psum_scatter(
            jnp.dot(context, full_o, preferred_element_type=jnp.float32),
            "tensor",
            scatter_dimension=0,
            tiled=True,
        )
        first_sum = own_rows.astype(jnp.float32) + attn_rows + b_o
        hidden, normed_one, factor_one = norm_rows(first_sum, gain_one, shift_one)
        hidden_low = hidden.astype(jnp.bfloat16)
        spread = lax.all_gather(hidden_low, "tensor", axis=0, tiled=True)
        upward = jnp.dot(spread, full_up, preferred_element_type=jnp.float32) + bias_up
        active = gelu_exact(upward).astype(jnp.bfloat16)
        ffn_rows = lax.psum_scatter(
            jnp.dot(active, full_down, preferred_element_type=jnp.float32),
            "tensor",
            scatter_dimension=0,
            tiled=True,
        )
        second_sum = hidden + ffn_rows + b_down
        result, normed_two, factor_two = norm_rows(second_sum, gain_two, shift_two)
        grad_out = out_grad[micro_index, 0].astype(jnp.float32)
        sum_g2 = jnp.sum(grad_out * normed_two, axis=0)
        sum_e2 = jnp.sum(grad_out, axis=0)
        grad_second = norm_back(grad_out, normed_two, factor_two, gain_two)
        sum_down = jnp.sum(grad_second, axis=0)
        second_low = grad_second.astype(jnp.bfloat16)
        grad_ffn = lax.all_gather(second_low, "tensor", axis=0, tiled=True)
        local_down = lax.dot_general(
            active, grad_ffn, (((0,), (0,)), ((), ())), preferred_element_type=jnp.float32
        )
        grad_active = lax.dot_general(
            grad_ffn, full_down, (((1,), (1,)), ((), ())), preferred_element_type=jnp.float32
        )
        grad_up = (grad_active * gelu_slope(upward)).astype(jnp.bfloat16)
        sum_up = jnp.sum(grad_up.astype(jnp.float32), axis=0)
        local_up = lax.dot_general(
            spread, grad_up, (((0,), (0,)), ((), ())), preferred_element_type=jnp.float32
        )
        grad_hidden = grad_second + lax.psum_scatter(
            lax.dot_general(
                grad_up, full_up, (((1,), (1,)), ((), ())), preferred_element_type=jnp.float32
            ),
            "tensor",
            scatter_dimension=0,
            tiled=True,
        )
        sum_g1 = jnp.sum(grad_hidden * normed_one, axis=0)
        sum_e1 = jnp.sum(grad_hidden, axis=0)
        grad_first = norm_back(grad_hidden, normed_one, factor_one, gain_one)
        sum_o = jnp.sum(grad_first, axis=0)
        first_low = grad_first.astype(jnp.bfloat16)
        grad_attn = lax.all_gather(first_low, "tensor", axis=0, tiled=True)
        local_o = lax.dot_general(
            context, grad_attn, (((0,), (0,)), ((), ())), preferred_element_type=jnp.float32
        )
        grad_context = lax.dot_general(
            grad_attn, full_o, (((1,), (1,)), ((), ())), preferred_element_type=jnp.float32
        ).astype(jnp.bfloat16)
        grad_q, grad_k, grad_v = attend_back(
            queries,
            key_rows,
            values,
            grad_context,
            logsum,
            seg_full,
            keep_full,
            score_scale,
            block_rows,
        )
        grad_proj = jnp.stack([grad_q, grad_k, grad_v])
        sum_qv = jnp.stack(
            [
                jnp.sum(grad_q.astype(jnp.float32), axis=0),
                jnp.sum(grad_v.astype(jnp.float32), axis=0),
            ]
        )
        local_qkv = jnp.einsum(
            "ld,cle->cde", gathered, grad_proj, preferred_element_type=jnp.float32
        )
        x_rows = grad_first + lax.psum_scatter(
            jnp.einsum(
                "cle,cde->ld", grad_proj, full_qkv, preferred_element_type=jnp.float32
            ).astype(jnp.bfloat16),
            "tensor",
            scatter_dimension=0,
            tiled=True,
        ).astype(jnp.float32)
        smalls = (sum_qv, sum_o, sum_g1, sum_e1, sum_up, sum_down, sum_g2, sum_e2)
        result, x_rows, local_grads, smalls = (
            result.astype(jnp.bfloat16),
            x_rows,
            (local_qkv, local_o, local_up, local_down),
            smalls,
        )
        out_list.append(result)
        grad_list.append(x_rows)
        small_totals = smalls if small_totals is None else add_all(small_totals, smalls)
        take_shard_grads = shard_grads
        settled = (
            lax.psum_scatter(local_grads[0], "dp", scatter_dimension=1, tiled=True),
            lax.psum_scatter(local_grads[1], "dp", scatter_dimension=1, tiled=True),
            lax.psum_scatter(local_grads[2], "dp", scatter_dimension=0, tiled=True),
            lax.psum_scatter(local_grads[3], "dp", scatter_dimension=1, tiled=True),
        )
        take_shard_grads = (
            settled if take_shard_grads is None else add_all(take_shard_grads, settled)
        )
        shard_grads, local_totals = (take_shard_grads, local_totals)
    out_rows = jnp.stack(out_list)[:, None]
    grad_rows = jnp.stack(grad_list)[:, None]
    qv_full = lax.dynamic_update_slice(
        jnp.zeros((2, half_width * tensor_count), jnp.float32),
        small_totals[0],
        (jnp.int32(0), tensor_rank * half_width),
    )
    up_full = lax.dynamic_update_slice(
        jnp.zeros((half_units * tensor_count,), jnp.float32),
        small_totals[4],
        (tensor_rank * half_units,),
    )
    summed = lax.psum(
        (
            qv_full,
            small_totals[1],
            small_totals[2],
            small_totals[3],
            up_full,
            small_totals[5],
            small_totals[6],
            small_totals[7],
        ),
        ("dp", "tensor"),
    )
    grad_qv = lax.dynamic_slice_in_dim(summed[0], tensor_rank * half_width, half_width, 1)
    grad_up_bias = lax.dynamic_slice_in_dim(summed[4], tensor_rank * half_units, half_units, 0)
    return (
        out_rows,
        grad_rows,
        shard_grads[0],
        grad_qv,
        shard_grads[1],
        summed[1],
        summed[2],
        summed[3],
        shard_grads[2],
        grad_up_bias,
        shard_grads[3],
        summed[5],
        summed[6],
        summed[7],
    )


def solution(mesh):
    placed = (
        P(None, "dp", "tensor", None),
        P(None, "dp", None),
        P(None, "dp", None),
        P(None, "dp", "tensor"),
        P(),
        P("tensor", "dp"),
        P(),
        P(),
        P(),
        P("dp", "tensor"),
        P(),
        P("tensor", "dp"),
        P(),
        P(),
        P(),
        P(None, "dp", "tensor", None),
    )
    return jax.shard_map(
        shards,
        mesh=mesh,
        in_specs=placed,
        out_specs=(
            P(None, "dp", "tensor", None),
            P(None, "dp", "tensor", None),
            P(None, "dp", "tensor"),
            P(None, "tensor"),
            P("tensor", "dp"),
            P(),
            P(),
            P(),
            P("dp", "tensor"),
            P("tensor"),
            P("tensor", "dp"),
            P(),
            P(),
            P(),
        ),
        check_vma=False,
    )
```

profile of v0, /device:TPU:0, one launch (start us, length us, event | category | flops | bytes accessed | tf_op | source)
XLA Modules:
  0.0 1215.2 jit_solution(6514101610812780588)
XLA Ops:
  11.5 24.9 %all_gather.42 = bf16[384,768]{0,1:T(8,128)(2,1)S(1)} all-gather(bf16[384,48]{0,1:T(8,128)(2,1)S(1)} %copy-done.58), channel_id=1, replica_groups=mesh['dp'=16,'tensor'=2] {'dp'}, dimensions={1}, use_global_device_ids=true | all-gather | bytes 626688 | tf_op jit(solution)/shard_map/all_gather | solution.py:180
  40.1 42.8 %all-gather.14.cloned.1.call-done = bf16[3,768,384]{2,1,0:T(8,128)(2,1)} async-done(((bf16[3,48,384]{2,1,0:T(8,128)(2,1)}), bf16[3,768,384]{2,1,0:T(8,128)(2,1)}) %all-gather.14.cloned.1.call-update) | async-done | bytes 1769488 | tf_op jit(solution)/shard_map/all_gather | solution.py:179
  90.9 26.0 %while.55 = (s32[]{:T(128)}, bf16[2,512,6,64]{1,3,2,0:T(8,128)(2,1)}, f32[2,6,512]{2,1,0:T(8,128)S(1)}, s32[2,512]{1,0:T(2,128)S(1)}, s32[1,1,1024]{2,1,0:T(1,12...) while((s32[]{:T(128)}, ...), condition=%wide.region_13.14_spmd, body=%wide.region_10.13_spmd.sunk | while | flops 845347328 | bytes 42336904 | solution.py:73
  132.2 26.0 %while.54 = (s32[]{:T(128)}, bf16[2,512,6,64]{1,3,2,0:T(8,128)(2,1)}, f32[2,6,512]{2,1,0:T(8,128)S(1)}, s32[2,512]{1,0:T(2,128)S(1)}, s32[1,1,1024]{2,1,0:T(1,12...) while((s32[]{:T(128)}, ...), condition=%wide.region_3.4_spmd, body=%wide.region_0.3_spmd.sunk | while | flops 845347328 | bytes 42336904 | solution.py:73
  165.5 46.1 %reduce-scatter.12.cloned.1.call-done = f32[512,768]{1,0:T(8,128)} async-done(((f32[1024,768]{1,0:T(8,128)}), f32[512,768]{1,0:T(8,128)}) %reduce-scatter.12.cloned.1.call-update) | async-done | bytes 1572880 | tf_op jit(solution)/shard_map/reduce_scatter | solution.py:196
  218.6 37.5 %all-gather.18.cloned.1.call-done = bf16[768,1536]{1,0:T(8,128)(2,1)} async-done(((bf16[48,1536]{1,0:T(8,128)(2,1)}), bf16[768,1536]{1,0:T(8,128)(2,1)}) %all-gather.18.cloned.1.call-update) | async-done | bytes 2359312 | tf_op jit(solution)/shard_map/all_gather | solution.py:181
  256.1 27.5 %all-gather.22.cloned.1.call-done = bf16[1024,768]{1,0:T(8,128)(2,1)} async-done(((bf16[512,768]{1,0:T(8,128)(2,1)}), bf16[1024,768]{1,0:T(8,128)(2,1)}) %all-gather.22.cloned.1.call-update) | async-done | bytes 1572880 | tf_op jit(solution)/shard_map/all_gather | solution.py:205
  283.6 7.4 fusion.149
  291.0 21.9 %all-gather.16.cloned.1.call-done = bf16[1024,768]{1,0:T(8,128)(2,1)} async-done(((bf16[512,768]{1,0:T(8,128)(2,1)}), bf16[1024,768]{1,0:T(8,128)(2,1)}) %all-gather.16.cloned.1.call-update) | async-done | bytes 1572880 | tf_op jit(solution)/shard_map/all_gather | solution.py:205
  312.9 11.0 multiply_convert_fusion.3
  324.0 33.6 %all-gather.20.cloned.1.call-done = bf16[1536,768]{0,1:T(8,128)(2,1)} async-done(((bf16[1536,48]{0,1:T(8,128)(2,1)}), bf16[1536,768]{0,1:T(8,128)(2,1)}) %all-gather.20.cloned.1.call-update) | async-done | bytes 2359312 | tf_op jit(solution)/shard_map/all_gather | solution.py:182
  357.6 6.9 fusion.147
  364.5 6.9 fusion.150
  371.5 35.3 %reduce-scatter.14.cloned.1.call-done = f32[512,768]{1,0:T(8,128)} async-done(((f32[1024,768]{1,0:T(8,128)}), f32[512,768]{1,0:T(8,128)}) %reduce-scatter.14.cloned.1.call-update) | async-done | bytes 1572880 | tf_op jit(solution)/shard_map/reduce_scatter | solution.py:208
  406.8 45.7 %reduce-scatter.18.cloned.1.call-done = f32[512,768]{1,0:T(8,128)} async-done(((f32[1024,768]{1,0:T(8,128)}), f32[512,768]{1,0:T(8,128)}) %reduce-scatter.18.cloned.1.call-update) | async-done | bytes 1572880 | tf_op jit(solution)/shard_map/reduce_scatter | solution.py:208
  467.6 24.7 %all-gather.24.cloned.1.call-done = bf16[1024,768]{1,0:T(8,128)(2,1)} async-done(((bf16[512,768]{1,0:T(8,128)(2,1)}), bf16[1024,768]{1,0:T(8,128)(2,1)}) %all-gather.24.cloned.1.call-update) | async-done | bytes 1572880 | tf_op jit(solution)/shard_map/all_gather | solution.py:222
  492.2 7.7 convert_reduce_fusion.1
  505.9 15.0 %all-gather.28.cloned.1.call-done = bf16[1024,768]{1,0:T(8,128)(2,1)} async-done(((bf16[512,768]{1,0:T(8,128)(2,1)}), bf16[1024,768]{1,0:T(8,128)(2,1)}) %all-gather.28.cloned.1.call-update) | async-done | bytes 1572880 | tf_op jit(solution)/shard_map/all_gather | solution.py:222
  521.0 7.7 convert_reduce_fusion
  534.7 31.8 %reduce-scatter.20.cloned.1.call-done = f32[512,768]{1,0:T(8,128)} async-done(((f32[1024,768]{1,0:T(8,128)}), f32[512,768]{1,0:T(8,128)}) %reduce-scatter.20.cloned.1.call-update) | async-done | bytes 1572880 | tf_op jit(solution)/shard_map/reduce_scatter | solution.py:234
  571.3 40.8 %reduce-scatter.24.cloned.1.call-done = f32[512,768]{1,0:T(8,128)} async-done(((f32[1024,768]{1,0:T(8,128)}), f32[512,768]{1,0:T(8,128)}) %reduce-scatter.24.cloned.1.call-update) | async-done | bytes 1572880 | tf_op jit(solution)/shard_map/reduce_scatter | solution.py:234
  624.0 22.5 %all-gather.26.cloned.1.call-done = bf16[1024,768]{1,0:T(8,128)(2,1)} async-done(((bf16[512,768]{1,0:T(8,128)(2,1)}), bf16[1024,768]{1,0:T(8,128)(2,1)}) %all-gather.26.cloned.1.call-update) | async-done | bytes 1572880 | tf_op jit(solution)/shard_map/all_gather | solution.py:247
  651.7 65.0 %while.56 = (s32[]{:T(128)}, f32[1024,6,64]{0,2,1:T(8,128)}, f32[1024,6,64]{0,2,1:T(8,128)}, bf16[2,512,6,64]{1,3,2,0:T(8,128)(2,1)}, bf16[2,512,6,64]{1,3,2,0:T...) while((s32[]{:T(128)}, f32[1024,6,64]{0,2,1:T(8,128)}, ...), condition=%wide.region_27.28_spmd.clone, body=%wide.region_25.27_spmd.clone.sunk | while | flops 2064906752 | bytes 211006768 | solution.py:118
  655.8 6.3 multiply_reduce_fusion.14
  662.1 5.0 multiply_convert_fusion.6
  667.1 5.3 bitcast_add_fusion.8
  672.4 6.2 fusion.269
  687.4 6.3 multiply_reduce_fusion.14
  698.7 5.7 bitcast_add_fusion.8
  704.5 6.2 fusion.269
  710.7 6.0 bitcast_add_fusion.9
  725.1 65.3 %while.57 = (s32[]{:T(128)}, f32[1024,6,64]{0,2,1:T(8,128)}, f32[1024,6,64]{0,2,1:T(8,128)}, bf16[2,512,6,64]{1,3,2,0:T(8,128)(2,1)}, bf16[2,512,6,64]{1,3,2,0:T...) while((s32[]{:T(128)}, f32[1024,6,64]{0,2,1:T(8,128)}, ...), condition=%wide.region_36.37_spmd.clone, body=%wide.region_34.36_spmd.clone.sunk | while | flops 2064906752 | bytes 211006768 | solution.py:118
  729.4 6.3 multiply_reduce_fusion.15
  740.7 5.3 bitcast_add_fusion.10
  746.0 6.2 fusion.281
  761.0 6.3 multiply_reduce_fusion.15
  772.3 5.8 bitcast_add_fusion.10
  778.1 6.2 fusion.281
  784.2 6.0 bitcast_add_fusion.11
  814.9 5.2 bitcast_convert_fusion.1
  820.4 5.2 bitcast_convert_fusion
  857.5 41.0 %all-reduce.1 = (f32[2,768]{1,0:T(2,128)S(1)}, f32[768]{0:T(1024)}, f32[768]{0:T(1024)}, f32[768]{0:T(1024)}, f32[3072]{0:T(1024)S(1)}, /*index=5*/f32[768]{0:T(1024)}, f32[768]{0:T(1024)}, f32[768]{0:T(1024)}) all-reduce(f32[2,768]{1,0:T(2,128)S(1)} %fusion.125, ...), channel_id=1, replica_groups=mesh['dp'=16,'tensor'=2] {'dp','tensor'}, use_global_device_ids=true, to_apply=%region_44.45 | all-reduce | flops 9216 | bytes 73728 | tf_op jit(solution)/shard_map/psum | solution.py:316
  899.8 31.1 %all-reduce.4.cloned.1.call-done = f32[3,768,384]{2,0,1:T(4,128)} async-done(((f32[3,768,384]{2,0,1:T(4,128)}), f32[3,768,384]{2,0,1:T(4,128)}) %all-reduce.4.cloned.1.call-update) | async-done | bytes 3538960
  932.6 26.5 %reduce-scatter.22.cloned.1.call-done = bf16[512,768]{1,0:T(8,128)(2,1)} async-done(((bf16[1024,768]{1,0:T(8,128)(2,1)}), bf16[512,768]{1,0:T(8,128)(2,1)}) %reduce-scatter.22.cloned.1.call-update) | async-done | bytes 786448 | tf_op jit(solution)/shard_map/reduce_scatter | solution.py:275
  961.5 25.9 %reduce-scatter.26.cloned.1.call-done = bf16[512,768]{1,0:T(8,128)(2,1)} async-done(((bf16[1024,768]{1,0:T(8,128)(2,1)}), bf16[512,768]{1,0:T(8,128)(2,1)}) %reduce-scatter.26.cloned.1.call-update) | async-done | bytes 786448 | tf_op jit(solution)/shard_map/reduce_scatter | solution.py:275
  990.6 76.7 %reduce-scatter.32.cloned.1.call-done = f32[1536,48]{0,1:T(8,128)} async-done(((f32[1536,768]{0,1:T(8,128)}), f32[1536,48]{0,1:T(8,128)}) %reduce-scatter.32.cloned.1.call-update) | async-done | bytes 294928 | tf_op jit(solution)/shard_map/reduce_scatter | solution.py:298
  1067.4 79.2 %reduce-scatter.30.cloned.1.call-done = f32[48,1536]{1,0:T(8,128)} async-done(((f32[768,1536]{1,0:T(8,128)}), f32[48,1536]{1,0:T(8,128)}) %reduce-scatter.30.cloned.1.call-update) | async-done | bytes 294928 | tf_op jit(solution)/shard_map/reduce_scatter | solution.py:297
  1146.6 61.6 %reduce-scatter.28.cloned.1.call-done = f32[384,48]{0,1:T(8,128)} async-done(((f32[384,768]{0,1:T(8,128)}), f32[384,48]{0,1:T(8,128)}) %reduce-scatter.28.cloned.1.call-update) | async-done | bytes 73744 | tf_op jit(solution)/shard_map/reduce_scatter | solution.py:296
  (439 shorter events, 258.3 us)
Async XLA Ops:
  7.2 29.3 %copy-start.80 = (f32[2,768]{1,0:T(2,128)S(1)}, f32[2,768]{1,0:T(2,128)}, u32[]{:S(2)}) copy-start(f32[2,768]{1,0:T(2,128)} %param.28) | copy-start | bytes 18436
  7.2 32.9 %all-gather.34.cloned.1.call-start = ((), (), s32[]{:S(2)}) async-start(), calls=%async_computation.29 | async-start | bytes 2359296 | tf_op jit(solution)/shard_map/all_gather | solution.py:184
  9.9 73.0 %all-gather.14.cloned.1.call-start = ((), (), s32[]{:S(2)}) async-start(), calls=%async_computation.11 | async-start | bytes 1880064 | tf_op jit(solution)/shard_map/all_gather | solution.py:179
  10.7 112.9 %all-gather.32.cloned.1.call-start = ((), (), s32[]{:S(2)}) async-start(), calls=%async_computation.28 | async-start | bytes 2359296 | tf_op jit(solution)/shard_map/all_gather | solution.py:184
  11.4 154.1 %reduce-scatter.16.cloned.1.call-start = ((), (), s32[]{:S(2)}) async-start(), calls=%async_computation.17 | async-start | bytes 4718592 | tf_op jit(solution)/shard_map/reduce_scatter | solution.py:196
  36.4 83.3 %copy-start.29 = (bf16[384,768]{0,1:T(8,128)(2,1)}, bf16[384,768]{0,1:T(8,128)(2,1)S(1)}, u32[]{:S(2)}) copy-start(bf16[384,768]{0,1:T(8,128)(2,1)S(1)} %all_gather.42) | copy-start | bytes 1769476
  116.9 6.3 copy-start.4
  116.9 6.3 copy-start.8
  116.9 6.3 copy-start.11
  117.0 6.3 copy-start.49
  123.3 88.4 %reduce-scatter.12.cloned.1.call-start = ((), (), s32[]{:S(2)}) async-start(), calls=%async_computation.12 | async-start | bytes 4718592 | tf_op jit(solution)/shard_map/reduce_scatter | solution.py:196
  164.2 47.4 %copy-start.77 = (f32[768]{0:T(1024)S(1)}, f32[768]{0:T(1024)}, u32[]{:S(2)}) copy-start(f32[768]{0:T(1024)} %param.30) | copy-start | bytes 9220
  164.3 91.8 %all-gather.18.cloned.1.call-start = ((), (), s32[]{:S(2)}) async-start(), calls=%async_computation.14 | async-start | bytes 2506752 | tf_op jit(solution)/shard_map/all_gather | solution.py:181
  164.8 118.7 %all-gather.22.cloned.1.call-start = ((), (), s32[]{:S(2)}) async-start(), calls=%async_computation.18 | async-start | bytes 2359296 | tf_op jit(solution)/shard_map/all_gather | solution.py:205
  217.0 95.9 %all-gather.16.cloned.1.call-start = ((), (), s32[]{:S(2)}) async-start(), calls=%async_computation.13 | async-start | bytes 2359296 | tf_op jit(solution)/shard_map/all_gather | solution.py:205
  217.7 139.8 %all-gather.20.cloned.1.call-start = ((), (), s32[]{:S(2)}) async-start(), calls=%async_computation.15 | async-start | bytes 2506752 | tf_op jit(solution)/shard_map/all_gather | solution.py:182
  218.5 188.3 %reduce-scatter.14.cloned.1.call-start = ((), (), s32[]{:S(2)}) async-start(), calls=%async_computation.16 | async-start | bytes 4718592 | tf_op jit(solution)/shard_map/reduce_scatter | solution.py:208
  364.5 88.0 %reduce-scatter.18.cloned.1.call-start = ((), (), s32[]{:S(2)}) async-start(), calls=%async_computation.19 | async-start | bytes 4718592 | tf_op jit(solution)/shard_map/reduce_scatter | solution.py:208
  371.4 81.1 %copy-start.78 = (f32[768]{0:T(1024)S(1)}, f32[768]{0:T(1024)}, u32[]{:S(2)}) copy-start(f32[768]{0:T(1024)} %param.36) | copy-start | bytes 9220
  371.5 120.8 %all-gather.24.cloned.1.call-start = ((), (), s32[]{:S(2)}) async-start(), calls=%async_computation.20 | async-start | bytes 2359296 | tf_op jit(solution)/shard_map/all_gather | solution.py:222
  464.9 56.1 %all-gather.28.cloned.1.call-start = ((), (), s32[]{:S(2)}) async-start(), calls=%async_computation.24 | async-start | bytes 2359296 | tf_op jit(solution)/shard_map/all_gather | solution.py:222
  467.3 99.2 %reduce-scatter.20.cloned.1.call-start = ((), (), s32[]{:S(2)}) async-start(), calls=%async_computation.21 | async-start | bytes 4718592 | tf_op jit(solution)/shard_map/reduce_scatter | solution.py:234
  492.2 9.3 copy-start.81
  505.9 106.2 %reduce-scatter.24.cloned.1.call-start = ((), (), s32[]{:S(2)}) async-start(), calls=%async_computation.25 | async-start | bytes 4718592 | tf_op jit(solution)/shard_map/reduce_scatter | solution.py:234
  521.0 9.4 copy-start.82
  534.7 111.9 %all-gather.26.cloned.1.call-start = ((), (), s32[]{:S(2)}) async-start(), calls=%async_computation.22 | async-start | bytes 2359296 | tf_op jit(solution)/shard_map/all_gather | solution.py:247
  619.2 100.6 %all-gather.30.cloned.1.call-start = ((), (), s32[]{:S(2)}) async-start(), calls=%async_computation.26 | async-start | bytes 2359296 | tf_op jit(solution)/shard_map/all_gather | solution.py:247
  621.8 24.7 %copy-start.31 = (bf16[384,768]{0,1:T(8,128)(2,1)S(1)}, bf16[384,768]{0,1:T(8,128)(2,1)}, u32[]{:S(2)}) copy-start(bf16[384,768]{0,1:T(8,128)(2,1)} %copy-done.29) | copy-start | bytes 1769476
  624.0 306.9 %all-reduce.4.cloned.1.call-start = ((), (), s32[]{:S(2)}) async-start(), calls=%async_computation.33 | async-start | bytes 9437184
  655.8 6.3 copy-start
  667.1 11.5 copy-start.1
  687.4 6.3 copy-start
  698.7 12.0 copy-start.1
  704.5 6.3 copy-start.21
  729.3 6.3 copy-start.2
  740.7 11.5 copy-start.3
  760.9 6.3 copy-start.2
  772.3 12.0 copy-start.3
  813.5 6.8 copy-start.42
  813.6 6.8 copy-start.44
  813.6 145.5 %reduce-scatter.22.cloned.1.call-start = ((), (), s32[]{:S(2)}) async-start(), calls=%async_computation.23 | async-start | bytes 2359296 | tf_op jit(solution)/shard_map/reduce_scatter | solution.py:275
  820.1 167.3 %reduce-scatter.26.cloned.1.call-start = ((), (), s32[]{:S(2)}) async-start(), calls=%async_computation.27 | async-start | bytes 2359296 | tf_op jit(solution)/shard_map/reduce_scatter | solution.py:275
  825.7 241.7 %reduce-scatter.32.cloned.1.call-start = ((), (), s32[]{:S(2)}) async-start(), calls=%async_computation.32 | async-start | bytes 5013504 | tf_op jit(solution)/shard_map/reduce_scatter | solution.py:298
  834.9 311.7 %reduce-scatter.30.cloned.1.call-start = ((), (), s32[]{:S(2)}) async-start(), calls=%async_computation.31 | async-start | bytes 5013504 | tf_op jit(solution)/shard_map/reduce_scatter | solution.py:297
  845.8 362.4 %reduce-scatter.28.cloned.1.call-start = ((), (), s32[]{:S(2)}) async-start(), calls=%async_computation.30 | async-start | bytes 1253376 | tf_op jit(solution)/shard_map/reduce_scatter | solution.py:296
  856.3 102.8 %copy-start.19 = (f32[512,768]{1,0:T(8,128)S(1)}, f32[512,768]{1,0:T(8,128)}, u32[]{:S(2)}) copy-start(f32[512,768]{1,0:T(8,128)} %copy-done.18) | copy-start | bytes 4718596
  931.9 55.5 %copy-start.17 = (f32[512,768]{1,0:T(8,128)S(1)}, f32[512,768]{1,0:T(8,128)}, u32[]{:S(2)}) copy-start(f32[512,768]{1,0:T(8,128)} %copy-done.16) | copy-start | bytes 4718596
  961.5 27.2 %copy-start.28 = (f32[1,512,768]{2,1,0:T(8,128)S(1)}, f32[1,512,768]{2,1,0:T(8,128)}, u32[]{:S(2)}) copy-start(f32[1,512,768]{2,1,0:T(8,128)} %add_bitcast_fusion.2) | copy-start | bytes 4718596
  (73 other events, 202.6 us)
Sparse Core Ops, SparseCore 0:
  10.1 29.8 all-gather.33
  42.4 40.4 all-gather.13
  85.0 25.8 all-gather.31
  123.4 42.0 reduce-scatter.15
  168.2 43.4 reduce-scatter.11
  213.8 42.3 all-gather.17
  257.7 25.8 all-gather.21
  285.7 27.1 all-gather.15
  315.2 42.2 all-gather.19
  364.6 42.1 reduce-scatter.13
  409.0 43.4 reduce-scatter.17
  465.0 27.1 all-gather.23
  493.8 27.1 all-gather.27
  523.1 43.4 reduce-scatter.19
  568.6 43.4 reduce-scatter.23
  619.3 27.1 all-gather.25
  647.9 27.1 all-gather.29
  813.7 117.1 all-reduce.3
  933.1 25.9 reduce-scatter.21
  961.1 26.1 reduce-scatter.25
  991.8 75.5 reduce-scatter.31
  1071.8 74.7 reduce-scatter.29
  1150.8 57.3 reduce-scatter.27
where the time goes:
time: 1220 us
  waiting for transfers between devices  734 us (60%)
  matrix products  246 us (20%)
  other arithmetic  91.2 us (7%)
  blocking collectives  65.9 us (5%)
  local copies, waits for them, and re-layouts  59.4 us (5%)
  between operations  16.3 us (1%)
    reduce_scatter x2, waiting for transfers between devices, shards(): lax.psum_scatter(jnp.dot(active, full_down, preferred_element_type=jnp.fl...  81 us
    reduce_scatter x1, waiting for transfers between devices, shards(): lax.psum_scatter(local_grads[2], 'dp', scatter_dimension=0, tiled=True)  79.2 us
    reduce_scatter x1, waiting for transfers between devices, shards(): lax.psum_scatter(local_grads[3], 'dp', scatter_dimension=1, tiled=True)  76.7 us
    reduce_scatter x2, waiting for transfers between devices, shards(): lax.psum_scatter(lax.dot_general(grad_up, full_up, (((1,), (1,)), ((), ()...  72.6 us
    reduce_scatter x1, waiting for transfers between devices, shards(): lax.psum_scatter(local_grads[1], 'dp', scatter_dimension=1, tiled=True)  61.6 us
    reduce_scatter x2, waiting for transfers between devices, shards(): lax.psum_scatter(jnp.einsum('cle,cde->ld', grad_proj, full_qkv, preferred...  52.3 us
    all_gather x2, waiting for transfers between devices, shards(): spread = lax.all_gather(hidden_low, 'tensor', axis=0, tiled=True)  49.4 us
    reduce_scatter x2, waiting for transfers between devices, shards(): lax.psum_scatter(jnp.dot(context, full_o, preferred_element_type=jnp.floa...  46.3 us
  transfers between devices with their start and end apart: 23, of which 21 were waited for; matrix products, arithmetic and copies ran while one was open for 22% of the time, Pallas kernels for 0%

commit v1 on v0

--- a/solution.py
+++ b/solution.py
@@ -6,6 +6,12 @@
 
 HEAD_DIM = 64
 EPS = 1e-06
+
+
+def joined_along(tiles, dim):
+    shape = list(tiles.shape[1:])
+    shape[dim] *= tiles.shape[0]
+    return jnp.moveaxis(tiles, 0, dim).reshape(shape)
 
 
 def gelu_exact(v):
@@ -178,7 +184,19 @@
         keep_full = keep_mask[micro_index, 0]
         full_qkv = lax.all_gather(w_qkv, "dp", axis=1, tiled=True)
         full_o = lax.all_gather(w_o, "dp", axis=1, tiled=True)
-        full_up = lax.all_gather(w_up, "dp", axis=0, tiled=True)
+        devices = lax.axis_size("dp")
+        pairs = [(i, (i + 1) % devices) for i in range(devices)]
+        back = [(b_2, a_2) for a_2, b_2 in pairs]
+        lower, upper = ([], [])
+        for lap in range(devices - 1):
+            if lap % 2 == 0:
+                lower.append(lax.ppermute(lower[-1] if lower else w_up, "dp", pairs))
+            else:
+                upper.append(lax.ppermute(upper[-1] if upper else w_up, "dp", back))
+        blocks = jnp.stack([*lower[::-1], w_up, *upper])
+        shift_2 = lax.axis_index("dp") - len(lower)
+        blocks = blocks[(jnp.arange(devices) - shift_2) % devices]
+        full_up = joined_along(blocks, 0)
         full_down = lax.all_gather(w_down, "dp", axis=1, tiled=True)
         head_count = full_qkv.shape[2] // HEAD_DIM
         gathered = lax.all_gather(own_rows, "tensor", axis=0, tiled=True)

time: 1220 us -> 1190 us (0.975)
  waiting for transfers between devices: 734 us -> 635 us
  starting transfers between devices: 1.94 us -> 34.7 us
  local copies, waits for them, and re-layouts: 59.4 us -> 86 us
    all_gather x2, waiting for transfers between devices: 49.4 us -> 0.01 us  [shards(): spread = lax.all_gather(hidden_low, 'tensor', axis=0, tiled=True)]
    all_gather x1 -> x0, waiting for transfers between devices: 37.5 us -> none  [shards(): full_up = lax.all_gather(w_up, 'dp', axis=0, tiled=True)]
    all_gather x1, waiting for transfers between devices: 33.6 us -> 0.01 us  [shards(): full_down = lax.all_gather(w_down, 'dp', axis=1, tiled=True)]
    ppermute x0 -> x15, starting transfers between devices: none -> 32.4 us  [the longest x7 32.3 us: shards(): upper.append(lax.ppermute(upper[-1] if upper else w_up, 'dp', back))]
    ppermute x0 -> x15, waiting for transfers between devices: none -> 26.1 us  [the longest x8 23.6 us: shards(): lower.append(lax.ppermute(lower[-1] if lower else w_up, 'dp', pairs))]
    unnamed x179 -> x208, local copies, waits for them, and re-layouts: 20.1 us -> 40 us
    unnamed x24 -> x23, waiting for transfers between devices: 34.7 us -> 32 us
  transfers between devices with their start and end apart: 23 -> 37, of which waited for: 21 -> 30; matrix products, arithmetic and copies ran while one was open for 22% -> 24% of each run, Pallas kernels for 0% -> 0%
where the time goes in v1:
time: 1190 us; the launch traced here: 1180 us
  waiting for transfers between devices  635 us (53%)
  matrix products  245 us (21%)
  other arithmetic  92.9 us (8%)
  local copies, waits for them, and re-layouts  86 us (7%)
  blocking collectives  66 us (6%)
  starting transfers between devices  34.7 us (3%)
  between operations  16.4 us (1%)
    reduce_scatter x1, waiting for transfers between devices, shards(): lax.psum_scatter(local_grads[2], 'dp', scatter_dimension=0, tiled=True)  79.2 us
    reduce_scatter x2, waiting for transfers between devices, shards(): lax.psum_scatter(jnp.dot(active, full_down, preferred_element_type=jnp.fl...  78.9 us
    reduce_scatter x1, waiting for transfers between devices, shards(): lax.psum_scatter(local_grads[3], 'dp', scatter_dimension=1, tiled=True)  76.6 us
    reduce_scatter x2, waiting for transfers between devices, shards(): lax.psum_scatter(lax.dot_general(grad_up, full_up, (((1,), (1,)), ((), ()...  72.7 us
    reduce_scatter x1, waiting for transfers between devices, shards(): lax.psum_scatter(local_grads[1], 'dp', scatter_dimension=1, tiled=True)  61.5 us
    reduce_scatter x2, waiting for transfers between devices, shards(): lax.psum_scatter(jnp.einsum('cle,cde->ld', grad_proj, full_qkv, preferred...  52.3 us
    reduce_scatter x2, waiting for transfers between devices, shards(): lax.psum_scatter(jnp.dot(context, full_o, preferred_element_type=jnp.floa...  46.8 us
    all_gather x1, waiting for transfers between devices, shards(): full_qkv = lax.all_gather(w_qkv, 'dp', axis=1, tiled=True)  42.8 us
  transfers between devices with their start and end apart: 37, of which 30 were waited for; matrix products, arithmetic and copies ran while one was open for 24% of the time, Pallas kernels for 0%

profile of v1, /device:TPU:0, one launch (start us, length us, event | category | flops | bytes accessed | tf_op | source)
XLA Modules:
  0.0 1177.2 jit_solution(9076344275766372239)
XLA Ops:
  11.5 24.9 %all_gather.38 = bf16[384,768]{0,1:T(8,128)(2,1)S(1)} all-gather(bf16[384,48]{0,1:T(8,128)(2,1)S(1)} %copy-done.67), channel_id=1, replica_groups=mesh['dp'=16,'tensor'=2] {'dp'}, dimensions={1}, use_global_device_ids=true | all-gather | bytes 626688 | tf_op jit(solution)/shard_map/all_gather | solution.py:186
  40.1 42.8 %all-gather.13.cloned.1.call-done = bf16[3,768,384]{2,1,0:T(8,128)(2,1)} async-done(((bf16[3,48,384]{2,1,0:T(8,128)(2,1)}), bf16[3,768,384]{2,1,0:T(8,128)(2,1)}) %all-gather.13.cloned.1.call-update) | async-done | bytes 1769488 | tf_op jit(solution)/shard_map/all_gather | solution.py:185
  90.9 26.0 %while.55 = (s32[]{:T(128)}, bf16[2,512,6,64]{1,3,2,0:T(8,128)(2,1)}, f32[2,6,512]{2,1,0:T(8,128)S(1)}, s32[2,512]{1,0:T(2,128)S(1)}, s32[1,1,1024]{2,1,0:T(1,12...) while((s32[]{:T(128)}, ...), condition=%wide.region_13.14_spmd, body=%wide.region_10.13_spmd.sunk | while | flops 845347328 | bytes 42336904 | solution.py:79
  132.2 26.0 %while.54 = (s32[]{:T(128)}, bf16[2,512,6,64]{1,3,2,0:T(8,128)(2,1)}, f32[2,6,512]{2,1,0:T(8,128)S(1)}, s32[2,512]{1,0:T(2,128)S(1)}, s32[1,1,1024]{2,1,0:T(1,12...) while((s32[]{:T(128)}, ...), condition=%wide.region_3.4_spmd, body=%wide.region_0.3_spmd.sunk | while | flops 845347328 | bytes 42336904 | solution.py:79
  165.5 46.1 %reduce-scatter.12.cloned.1.call-done = f32[512,768]{1,0:T(8,128)} async-done(((f32[1024,768]{1,0:T(8,128)}), f32[512,768]{1,0:T(8,128)}) %reduce-scatter.12.cloned.1.call-update) | async-done | bytes 1572880 | tf_op jit(solution)/shard_map/reduce_scatter | solution.py:214
  217.9 7.3 collective-permute-done
  300.9 7.4 fusion.151
  308.3 11.2 multiply_convert_fusion.3
  319.5 6.9 fusion.149
  326.5 6.9 fusion.152
  333.6 33.4 %reduce-scatter.14.cloned.1.call-done = f32[512,768]{1,0:T(8,128)} async-done(((f32[1024,768]{1,0:T(8,128)}), f32[512,768]{1,0:T(8,128)}) %reduce-scatter.14.cloned.1.call-update) | async-done | bytes 1572880 | tf_op jit(solution)/shard_map/reduce_scatter | solution.py:226
  367.0 45.6 %reduce-scatter.18.cloned.1.call-done = f32[512,768]{1,0:T(8,128)} async-done(((f32[1024,768]{1,0:T(8,128)}), f32[512,768]{1,0:T(8,128)}) %reduce-scatter.18.cloned.1.call-update) | async-done | bytes 1572880 | tf_op jit(solution)/shard_map/reduce_scatter | solution.py:226
  427.4 24.9 %all-gather.21.cloned.1.call-done = bf16[1024,768]{1,0:T(8,128)(2,1)} async-done(((bf16[512,768]{1,0:T(8,128)(2,1)}), bf16[1024,768]{1,0:T(8,128)(2,1)}) %all-gather.21.cloned.1.call-update) | async-done | bytes 1572880 | tf_op jit(solution)/shard_map/all_gather | solution.py:240
  452.3 7.7 convert_reduce_fusion.1
  466.0 14.8 %all-gather.25.cloned.1.call-done = bf16[1024,768]{1,0:T(8,128)(2,1)} async-done(((bf16[512,768]{1,0:T(8,128)(2,1)}), bf16[1024,768]{1,0:T(8,128)(2,1)}) %all-gather.25.cloned.1.call-update) | async-done | bytes 1572880 | tf_op jit(solution)/shard_map/all_gather | solution.py:240
  480.9 7.7 convert_reduce_fusion
  494.7 31.9 %reduce-scatter.20.cloned.1.call-done = f32[512,768]{1,0:T(8,128)} async-done(((f32[1024,768]{1,0:T(8,128)}), f32[512,768]{1,0:T(8,128)}) %reduce-scatter.20.cloned.1.call-update) | async-done | bytes 1572880 | tf_op jit(solution)/shard_map/reduce_scatter | solution.py:252
  531.3 40.8 %reduce-scatter.24.cloned.1.call-done = f32[512,768]{1,0:T(8,128)} async-done(((f32[1024,768]{1,0:T(8,128)}), f32[512,768]{1,0:T(8,128)}) %reduce-scatter.24.cloned.1.call-update) | async-done | bytes 1572880 | tf_op jit(solution)/shard_map/reduce_scatter | solution.py:252
  584.3 22.5 %all-gather.23.cloned.1.call-done = bf16[1024,768]{1,0:T(8,128)(2,1)} async-done(((bf16[512,768]{1,0:T(8,128)(2,1)}), bf16[1024,768]{1,0:T(8,128)(2,1)}) %all-gather.23.cloned.1.call-update) | async-done | bytes 1572880 | tf_op jit(solution)/shard_map/all_gather | solution.py:265
  612.0 65.1 %while.56 = (s32[]{:T(128)}, f32[1024,6,64]{0,2,1:T(8,128)}, f32[1024,6,64]{0,2,1:T(8,128)}, bf16[2,512,6,64]{1,3,2,0:T(8,128)(2,1)}, bf16[2,512,6,64]{1,3,2,0:T...) while((s32[]{:T(128)}, f32[1024,6,64]{0,2,1:T(8,128)}, ...), condition=%wide.region_27.28_spmd.clone, body=%wide.region_25.27_spmd.clone.sunk | while | flops 2064906752 | bytes 211006768 | solution.py:124
  616.2 6.3 multiply_reduce_fusion.14
  622.5 5.1 multiply_convert_fusion.6
  627.5 5.3 bitcast_add_fusion.8
  632.9 6.2 fusion.271
  647.8 6.3 multiply_reduce_fusion.14
  654.1 5.1 multiply_convert_fusion.6
  659.1 5.7 bitcast_add_fusion.8
  664.9 6.2 fusion.271
  671.1 6.0 bitcast_add_fusion.9
  685.4 65.1 %while.57 = (s32[]{:T(128)}, f32[1024,6,64]{0,2,1:T(8,128)}, f32[1024,6,64]{0,2,1:T(8,128)}, bf16[2,512,6,64]{1,3,2,0:T(8,128)(2,1)}, bf16[2,512,6,64]{1,3,2,0:T...) while((s32[]{:T(128)}, f32[1024,6,64]{0,2,1:T(8,128)}, ...), condition=%wide.region_36.37_spmd.clone, body=%wide.region_34.36_spmd.clone.sunk | while | flops 2064906752 | bytes 211006768 | solution.py:124
  689.4 6.3 multiply_reduce_fusion.15
  695.7 5.1 multiply_convert_fusion.7
  700.8 5.3 bitcast_add_fusion.10
  706.1 6.2 fusion.283
  721.1 6.3 multiply_reduce_fusion.15
  727.3 5.1 multiply_convert_fusion.7
  732.4 5.7 bitcast_add_fusion.10
  738.1 6.2 fusion.283
  744.4 6.0 bitcast_add_fusion.11
  777.3 5.1 bitcast_convert_fusion.1
  782.9 5.2 bitcast_convert_fusion
  821.1 41.1 %all-reduce.1 = (f32[2,768]{1,0:T(2,128)S(1)}, f32[768]{0:T(1024)}, f32[768]{0:T(1024)}, f32[768]{0:T(1024)}, f32[3072]{0:T(1024)S(1)}, /*index=5*/f32[768]{0:T(1024)}, f32[768]{0:T(1024)}, f32[768]{0:T(1024)}) all-reduce(f32[2,768]{1,0:T(2,128)S(1)} %fusion.125, ...), channel_id=1, replica_groups=mesh['dp'=16,'tensor'=2] {'dp','tensor'}, use_global_device_ids=true, to_apply=%region_44.45 | all-reduce | flops 9216 | bytes 73728 | tf_op jit(solution)/shard_map/psum | solution.py:334
  863.5 29.6 %all-reduce.4.cloned.1.call-done = f32[3,768,384]{2,0,1:T(4,128)} async-done(((f32[3,768,384]{2,0,1:T(4,128)}), f32[3,768,384]{2,0,1:T(4,128)}) %all-reduce.4.cloned.1.call-update) | async-done | bytes 3538960
  894.8 26.3 %reduce-scatter.22.cloned.1.call-done = bf16[512,768]{1,0:T(8,128)(2,1)} async-done(((bf16[1024,768]{1,0:T(8,128)(2,1)}), bf16[512,768]{1,0:T(8,128)(2,1)}) %reduce-scatter.22.cloned.1.call-update) | async-done | bytes 786448 | tf_op jit(solution)/shard_map/reduce_scatter | solution.py:293
  923.6 26.0 %reduce-scatter.26.cloned.1.call-done = bf16[512,768]{1,0:T(8,128)(2,1)} async-done(((bf16[1024,768]{1,0:T(8,128)(2,1)}), bf16[512,768]{1,0:T(8,128)(2,1)}) %reduce-scatter.26.cloned.1.call-update) | async-done | bytes 786448 | tf_op jit(solution)/shard_map/reduce_scatter | solution.py:293
  952.9 76.6 %reduce-scatter.32.cloned.1.call-done = f32[1536,48]{0,1:T(8,128)} async-done(((f32[1536,768]{0,1:T(8,128)}), f32[1536,48]{0,1:T(8,128)}) %reduce-scatter.32.cloned.1.call-update) | async-done | bytes 294928 | tf_op jit(solution)/shard_map/reduce_scatter | solution.py:316
  1029.4 79.2 %reduce-scatter.30.cloned.1.call-done = f32[48,1536]{1,0:T(8,128)} async-done(((f32[768,1536]{1,0:T(8,128)}), f32[48,1536]{1,0:T(8,128)}) %reduce-scatter.30.cloned.1.call-update) | async-done | bytes 294928 | tf_op jit(solution)/shard_map/reduce_scatter | solution.py:315
  1108.7 61.5 %reduce-scatter.28.cloned.1.call-done = f32[384,48]{0,1:T(8,128)} async-done(((f32[384,768]{0,1:T(8,128)}), f32[384,48]{0,1:T(8,128)}) %reduce-scatter.28.cloned.1.call-update) | async-done | bytes 73744 | tf_op jit(solution)/shard_map/reduce_scatter | solution.py:314
  (499 shorter events, 322.2 us)
Async XLA Ops:
  7.2 29.3 %copy-start.89 = (f32[2,768]{1,0:T(2,128)S(1)}, f32[2,768]{1,0:T(2,128)}, u32[]{:S(2)}) copy-start(f32[2,768]{1,0:T(2,128)} %param.28) | copy-start | bytes 18436
  7.2 32.9 %all-gather.31.cloned.1.call-start = ((), (), s32[]{:S(2)}) async-start(), calls=%async_computation.28 | async-start | bytes 2359296 | tf_op jit(solution)/shard_map/all_gather | solution.py:202
  9.9 73.0 %all-gather.13.cloned.1.call-start = ((), (), s32[]{:S(2)}) async-start(), calls=%async_computation.11 | async-start | bytes 1880064 | tf_op jit(solution)/shard_map/all_gather | solution.py:185
  10.7 113.0 %all-gather.29.cloned.1.call-start = ((), (), s32[]{:S(2)}) async-start(), calls=%async_computation.27 | async-start | bytes 2359296 | tf_op jit(solution)/shard_map/all_gather | solution.py:202
  11.4 154.1 %reduce-scatter.16.cloned.1.call-start = ((), (), s32[]{:S(2)}) async-start(), calls=%async_computation.16 | async-start | bytes 4718592 | tf_op jit(solution)/shard_map/reduce_scatter | solution.py:214
  36.4 83.3 %copy-start.29 = (bf16[384,768]{0,1:T(8,128)(2,1)}, bf16[384,768]{0,1:T(8,128)(2,1)S(1)}, u32[]{:S(2)}) copy-start(bf16[384,768]{0,1:T(8,128)(2,1)S(1)} %all_gather.38) | copy-start | bytes 1769476
  123.3 88.3 %reduce-scatter.12.cloned.1.call-start = ((), (), s32[]{:S(2)}) async-start(), calls=%async_computation.12 | async-start | bytes 4718592 | tf_op jit(solution)/shard_map/reduce_scatter | solution.py:214
  164.2 47.4 %copy-start.86 = (f32[768]{0:T(1024)S(1)}, f32[768]{0:T(1024)}, u32[]{:S(2)}) copy-start(f32[768]{0:T(1024)} %param.30) | copy-start | bytes 9220
  164.3 136.7 %all-gather.19.cloned.1.call-start = ((), (), s32[]{:S(2)}) async-start(), calls=%async_computation.17 | async-start | bytes 2359296 | tf_op jit(solution)/shard_map/all_gather | solution.py:223
  215.3 54.4 %copy-start.85 = (f32[3072]{0:T(1024)S(1)}, f32[3072]{0:T(1024)}, u32[]{:S(2)}) copy-start(f32[3072]{0:T(1024)} %param.34) | copy-start | bytes 36868
  217.0 91.3 %all-gather.15.cloned.1.call-start = ((), (), s32[]{:S(2)}) async-start(), calls=%async_computation.13 | async-start | bytes 2359296 | tf_op jit(solution)/shard_map/all_gather | solution.py:223
  217.8 101.7 %all-gather.17.cloned.1.call-start = ((), (), s32[]{:S(2)}) async-start(), calls=%async_computation.14 | async-start | bytes 2506752 | tf_op jit(solution)/shard_map/all_gather | solution.py:200
  217.8 7.3 collective-permute-start
  225.1 7.3 collective-permute-start.1
  225.1 7.3 collective-permute-start.8
  232.4 7.4 collective-permute-start.2
  233.1 7.1 collective-permute-start.9
  239.8 7.4 collective-permute-start.3
  240.2 7.4 collective-permute-start.10
  247.2 7.4 collective-permute-start.4
  247.6 7.4 collective-permute-start.11
  254.5 7.5 collective-permute-start.5
  254.9 7.8 collective-permute-start.12
  262.0 7.7 collective-permute-start.6
  262.0 105.0 %reduce-scatter.14.cloned.1.call-start = ((), (), s32[]{:S(2)}) async-start(), calls=%async_computation.15 | async-start | bytes 4718592 | tf_op jit(solution)/shard_map/reduce_scatter | solution.py:226
  262.7 7.7 collective-permute-start.13
  269.7 7.6 collective-permute-start.7
  269.7 20.6 %copy-start.60 = (bf16[48,1536]{1,0:T(8,128)(2,1)S(1)}, bf16[48,1536]{1,0:T(8,128)(2,1)}, u32[]{:S(2)}) copy-start(bf16[48,1536]{1,0:T(8,128)(2,1)} %copy-done.59) | copy-start | bytes 442372
  269.7 21.3 %copy-start.63 = (bf16[48,1536]{1,0:T(8,128)(2,1)S(1)}, bf16[48,1536]{1,0:T(8,128)(2,1)}, u32[]{:S(2)}) copy-start(bf16[48,1536]{1,0:T(8,128)(2,1)} %copy-done.62) | copy-start | bytes 442372
  270.4 26.0 %collective-permute-start.14 = (bf16[48,1536]{1,0:T(8,128)(2,1)}, bf16[48,1536]{1,0:T(8,128)(2,1)S(1)}, u32[]{:S(2)}, u32[]{:S(2)}) collective-permute-start(bf16[48,1536]{1,0:T(8,128)(2,1)} %collective-permute-done.13), channel_id=1, source_target_pairs={{2,0},{4,2},{6,4},{8,6},{10,8},{12,10},{14,12},{16,14},{18,16},{20... | collective-permute-start | bytes 442376 | tf_op jit(solution)/shard_map/ppermute | solution.py:195
  326.4 86.1 %reduce-scatter.18.cloned.1.call-start = ((), (), s32[]{:S(2)}) async-start(), calls=%async_computation.18 | async-start | bytes 4718592 | tf_op jit(solution)/shard_map/reduce_scatter | solution.py:226
  333.4 79.2 %copy-start.87 = (f32[768]{0:T(1024)S(1)}, f32[768]{0:T(1024)}, u32[]{:S(2)}) copy-start(f32[768]{0:T(1024)} %param.36) | copy-start | bytes 9220
  333.4 118.9 %all-gather.21.cloned.1.call-start = ((), (), s32[]{:S(2)}) async-start(), calls=%async_computation.19 | async-start | bytes 2359296 | tf_op jit(solution)/shard_map/all_gather | solution.py:240
  424.9 56.0 %all-gather.25.cloned.1.call-start = ((), (), s32[]{:S(2)}) async-start(), calls=%async_computation.23 | async-start | bytes 2359296 | tf_op jit(solution)/shard_map/all_gather | solution.py:240
  427.4 99.2 %reduce-scatter.20.cloned.1.call-start = ((), (), s32[]{:S(2)}) async-start(), calls=%async_computation.20 | async-start | bytes 4718592 | tf_op jit(solution)/shard_map/reduce_scatter | solution.py:252
  466.0 106.2 %reduce-scatter.24.cloned.1.call-start = ((), (), s32[]{:S(2)}) async-start(), calls=%async_computation.24 | async-start | bytes 4718592 | tf_op jit(solution)/shard_map/reduce_scatter | solution.py:252
  494.7 112.1 %all-gather.23.cloned.1.call-start = ((), (), s32[]{:S(2)}) async-start(), calls=%async_computation.21 | async-start | bytes 2359296 | tf_op jit(solution)/shard_map/all_gather | solution.py:265
  579.4 100.7 %all-gather.27.cloned.1.call-start = ((), (), s32[]{:S(2)}) async-start(), calls=%async_computation.25 | async-start | bytes 2359296 | tf_op jit(solution)/shard_map/all_gather | solution.py:265
  582.0 24.7 %copy-start.31 = (bf16[384,768]{0,1:T(8,128)(2,1)S(1)}, bf16[384,768]{0,1:T(8,128)(2,1)}, u32[]{:S(2)}) copy-start(bf16[384,768]{0,1:T(8,128)(2,1)} %copy-done.29) | copy-start | bytes 1769476
  584.2 308.9 %all-reduce.4.cloned.1.call-start = ((), (), s32[]{:S(2)}) async-start(), calls=%async_computation.32 | async-start | bytes 9437184
  775.9 145.2 %reduce-scatter.22.cloned.1.call-start = ((), (), s32[]{:S(2)}) async-start(), calls=%async_computation.22 | async-start | bytes 2359296 | tf_op jit(solution)/shard_map/reduce_scatter | solution.py:293
  782.4 167.2 %reduce-scatter.26.cloned.1.call-start = ((), (), s32[]{:S(2)}) async-start(), calls=%async_computation.26 | async-start | bytes 2359296 | tf_op jit(solution)/shard_map/reduce_scatter | solution.py:293
  788.1 241.4 %reduce-scatter.32.cloned.1.call-start = ((), (), s32[]{:S(2)}) async-start(), calls=%async_computation.31 | async-start | bytes 5013504 | tf_op jit(solution)/shard_map/reduce_scatter | solution.py:316
  797.3 311.3 %reduce-scatter.30.cloned.1.call-start = ((), (), s32[]{:S(2)}) async-start(), calls=%async_computation.30 | async-start | bytes 5013504 | tf_op jit(solution)/shard_map/reduce_scatter | solution.py:315
  808.1 362.1 %reduce-scatter.28.cloned.1.call-start = ((), (), s32[]{:S(2)}) async-start(), calls=%async_computation.29 | async-start | bytes 1253376 | tf_op jit(solution)/shard_map/reduce_scatter | solution.py:314
  817.1 104.0 %copy-start.19 = (f32[512,768]{1,0:T(8,128)S(1)}, f32[512,768]{1,0:T(8,128)}, u32[]{:S(2)}) copy-start(f32[512,768]{1,0:T(8,128)} %copy-done.18) | copy-start | bytes 4718596
  894.1 55.5 %copy-start.17 = (f32[512,768]{1,0:T(8,128)S(1)}, f32[512,768]{1,0:T(8,128)}, u32[]{:S(2)}) copy-start(f32[512,768]{1,0:T(8,128)} %copy-done.16) | copy-start | bytes 4718596
  923.6 27.3 %copy-start.28 = (f32[1,512,768]{2,1,0:T(8,128)S(1)}, f32[1,512,768]{2,1,0:T(8,128)}, u32[]{:S(2)}) copy-start(f32[1,512,768]{2,1,0:T(8,128)} %add_bitcast_fusion.2) | copy-start | bytes 4718596
  (94 other events, 411.7 us)
Sparse Core Ops, SparseCore 0:
  10.1 29.8 all-gather.30
  42.4 40.4 all-gather.12
  85.0 25.8 all-gather.28
  123.4 42.0 reduce-scatter.15
  168.2 43.3 reduce-scatter.11
  217.1 27.1 all-gather.18
  245.9 27.1 all-gather.14
  275.4 42.2 all-gather.16
  326.5 40.3 reduce-scatter.13
  369.1 43.4 reduce-scatter.17
  425.0 27.1 all-gather.20
  453.7 27.1 all-gather.24
  483.1 43.4 reduce-scatter.19
  528.7 43.4 reduce-scatter.23
  579.5 27.1 all-gather.22
  608.2 27.1 all-gather.26
  776.0 116.9 all-reduce.3
  895.2 25.9 reduce-scatter.21
  923.4 26.1 reduce-scatter.25
  953.8 75.5 reduce-scatter.31
  1033.9 74.7 reduce-scatter.29
  1112.8 57.3 reduce-scatter.27
